TPU v7x, 32 devices: a whole 2x2x4 slice. The times are simulated.
32 devices in a mesh: dp: 2 (over x), tp: 16 (over y, z, core).
Axes of the slice: x: 2, y: 2, z: 4, core: 2. Of those that a mesh axis runs over, the one named last changes fastest.
Arguments:
- x: bfloat16 [5120, 7168], P(('dp', 'tp')), parts along dimension 0
- w_gate: bfloat16 [7168, 20480], P(None, 'tp')
- w_up: bfloat16 [7168, 20480], P(None, 'tp')
- w_down: bfloat16 [20480, 7168], P('tp')
Outputs:
- output: bfloat16 [5120, 7168], P(('dp', 'tp')), parts along dimension 0
There are 2 independent parts. A program takes and returns all parts, laid end to end along the dimension named above; an argument that names none is the same for every part.
All inputs are finite; a program needn't handle non-finite values.
Results may differ from a plain program's by a relative error of at most 0.016.
Values are sent between devices in bfloat16 or wider.
A program may use at most 2 GiB of HBM per device.

v0:
```python
import jax
import jax.numpy as jnp
from jax import lax
from jax.sharding import PartitionSpec as P


def solution(mesh):
    def step(x, w_gate, w_up, w_down):
        rows = lax.all_gather(x, "tp", axis=0, tiled=True)
        gate = jnp.dot(rows, w_gate, preferred_element_type=jnp.float32)
        up = jnp.dot(rows, w_up, preferred_element_type=jnp.float32)
        hidden = (jax.nn.silu(gate) * up).astype(jnp.bfloat16)
        term = jnp.dot(hidden, w_down, preferred_element_type=jnp.float32).astype(jnp.bfloat16)
        return lax.psum_scatter(term, "tp", scatter_dimension=0, tiled=True)

    return jax.shard_map(
        step,
        mesh=mesh,
        in_specs=(P(("dp", "tp"), None), P(None, "tp"), P(None, "tp"), P("tp", None)),
        out_specs=P(("dp", "tp"), None),
        check_vma=False,
    )
```

profile of v0, /device:TPU:0, one launch (start us, length us, event | category | flops | bytes accessed | tf_op | source)
XLA Modules:
  0.0 727.1 jit_solution(16767525104695466078)
XLA Ops:
  6.5 0.0 all-gather.2.cloned.1.call-start
  6.5 0.7 all-gather.2.cloned.1.call-update
  7.3 0.0 reduce-scatter.2.cloned.1.call-start
  7.3 187.2 %all-gather.2.cloned.1.call-done = bf16[2560,7168]{1,0:T(8,128)(2,1)} async-done(((bf16[160,7168]{1,0:T(8,128)(2,1)}), bf16[2560,7168]{1,0:T(8,128)(2,1)}) %all-gather.2.cloned.1.call-update) | async-done | bytes 36700176 | tf_op jit(solution)/shard_map/all_gather | solution.py:9
  194.5 57.9 %fusion.1 = f32[2560,1280]{1,0:T(8,128)} fusion(bf16[2560,7168]{1,0:T(8,128)(2,1)} %all-gather.2.cloned.1.call-done, bf16[7168,1280]{1,0:T(8,128)(2,1)} %param.5), kind=kOutput, calls=%fused_computation.3 | convolution fusion | flops 46976204800 | bytes 68157440 | tf_op jit(solution)/shard_map/dot_general | solution.py:10
  252.3 57.7 %fusion = bf16[2560,1280]{1,0:T(8,128)(2,1)S(1)} fusion(bf16[2560,7168]{1,0:T(8,128)(2,1)} %all-gather.2.cloned.1.call-done, bf16[7168,1280]{1,0:T(8,128)(2,1)} %param.6, f32[2560,1280]{1,0:T(8,128)} %fusion.1), kind=kOutput, calls=%fused_computation.2 | convolution fusion | flops 46995865600 | bytes 74711040 | tf_op jit(solution)/shard_map/dot_general | solution.py:11
  310.0 56.5 %convolution_convert_fusion = bf16[2560,7168]{1,0:T(8,128)(2,1)} fusion(bf16[2560,1280]{1,0:T(8,128)(2,1)S(1)} %fusion, bf16[1280,7168]{1,0:T(8,128)(2,1)} %param.7), kind=kOutput, calls=%fused_computation | convolution fusion | flops 46994554880 | bytes 61603840 | tf_op jit(solution)/shard_map/dot_general | solution.py:13
  366.5 0.0 reduce-scatter.2.cloned.1.call-update
  366.5 353.8 %reduce-scatter.2.cloned.1.call-done = bf16[160,7168]{1,0:T(8,128)(2,1)} async-done(((bf16[2560,7168]{1,0:T(8,128)(2,1)}), bf16[160,7168]{1,0:T(8,128)(2,1)}) %reduce-scatter.2.cloned.1.call-update) | async-done | bytes 2293776 | tf_op jit(solution)/shard_map/reduce_scatter | solution.py:14
Async XLA Ops:
  6.5 187.9 %all-gather.2.cloned.1.call-start = ((), (), s32[]{:S(2)}) async-start(), calls=%async_computation.1 | async-start | bytes 38993920 | tf_op jit(solution)/shard_map/all_gather | solution.py:9
  7.3 713.0 %reduce-scatter.2.cloned.1.call-start = ((), (), s32[]{:S(2)}) async-start(), calls=%async_computation.2 | async-start | bytes 38993920 | tf_op jit(solution)/shard_map/reduce_scatter | solution.py:14
Sparse Core Ops, SparseCore 0:
  8.9 185.4 all-gather.1
  366.6 353.5 reduce-scatter.1
where the time goes:
time: 727 us
  waiting for transfers between devices  542 us (75%)
  matrix products  172 us (24%)
  between operations  13.4 us (2%)
    reduce_scatter x1, waiting for transfers between devices, step(): return lax.psum_scatter(term, 'tp', scatter_dimension=0, tiled=True)  354 us
    all_gather x1, waiting for transfers between devices, step(): rows = lax.all_gather(x, 'tp', axis=0, tiled=True)  187 us
    dot_general x1, matrix products, step(): gate = jnp.dot(rows, w_gate, preferred_element_type=jnp.float32)  57.9 us
    dot_general x1, matrix products, step(): up = jnp.dot(rows, w_up, preferred_element_type=jnp.float32)  57.7 us
    dot_general x1, matrix products, step(): jnp.dot(hidden, w_down, preferred_element_type=jnp.float32)  56.5 us
  transfers between devices with their start and end apart: 2, of which 2 were waited for; matrix products, arithmetic and copies ran while one was open for 0% of the time, Pallas kernels for 0%

commit v1 on v0

v1 whole, which is shorter than its diff:
```python
import jax
import jax.numpy as jnp
from jax import lax
from jax.experimental import pallas as pl
from jax.experimental.pallas import tpu as pltpu
from jax.sharding import PartitionSpec as P

MESH = pl.DeviceIdType.MESH
F32 = jnp.float32
BF16 = jnp.bfloat16
RING = 8
TF = 256
TN = 1024


def chip_at(place):
    y = lax.div(place, 4)
    along = lax.rem(place, 4)
    return 4 * y + along + y * (3 - 2 * along)


def kernel(x_ref, wg_ref, wu_ref, wd_ref, y_ref, xg_ref, xbuf, wgbuf, wubuf, wdbuf, hid, acc, rs, d2d, pbuf, sbuf,
           ag_send, ag_recv, xd_send, xd_recv, rs_send, rs_recv, dd_send, dd_recv, x_sem, wgu_sem, wd_sem, y_sem):
    rows = x_ref.shape[0]
    half = rows // 2
    nf = wg_ref.shape[1] // TF
    nn = wd_ref.shape[1] // TN
    me = lax.axis_index("tp")
    chip = lax.div(me, 2)
    core = lax.rem(me, 2)
    y, z = lax.div(chip, 4), lax.rem(chip, 4)
    place = z + y * (7 - 2 * z)
    nxt = chip_at(lax.rem(place + 1, RING)) * 2 + core
    prv = chip_at(lax.rem(place + RING - 1, RING)) * 2 + core
    partner = chip * 2 + 1 - core
    to = (nxt, prv)

    barrier = pltpu.get_barrier_semaphore()
    for other in (nxt, prv, partner):
        pl.semaphore_signal(barrier, inc=1, device_id={"tp": other}, device_id_type=MESH)
    pl.semaphore_wait(barrier, 3)

    def part(d):
        return pl.ds(d * half, half)

    def remote(src, dst, send, recv, dev):
        return pltpu.make_async_remote_copy(
            src_ref=src, dst_ref=dst, send_sem=send, recv_sem=recv, device_id={"tp": dev}, device_id_type=MESH)

    def ag(s, d, first=False):
        src = x_ref.at[part(d)] if first else xg_ref.at[s - 1, part(d)]
        return remote(src, xg_ref.at[s, part(d)], ag_send.at[s, d], ag_recv.at[s, d], to[d])

    def xd(s, own=False):
        src = x_ref if own else xg_ref.at[s - 1, pl.ds(0, rows)]
        return remote(src, xg_ref.at[s - 1, pl.ds(rows, rows)], xd_send.at[s - 1], xd_recv.at[s - 1], partner)

    def rsc(s, n, d):
        return remote(sbuf.at[lax.rem(s, 2), n, part(d)], rs.at[lax.rem(s + 1, 3), n, part(d)],
                      rs_send.at[lax.rem(s, 2), n, d], rs_recv.at[lax.rem(s + 1, 3), n, d], to[d])

    def rs_in(s, n, d):
        return remote(sbuf.at[0, n, part(d)], rs.at[lax.rem(s, 3), n, part(d)],
                      rs_send.at[0, n, d], rs_recv.at[lax.rem(s, 3), n, d], to[d])

    def dd(n):
        return remote(pbuf.at[n], d2d.at[n], dd_send.at[n], dd_recv.at[n], partner)

    def wgu(i):
        t, slot = lax.rem(i, nf), lax.rem(i, 2)
        cols = pl.ds(pl.multiple_of(t * TF, TF), TF)
        return (pltpu.make_async_copy(wg_ref.at[:, cols], wgbuf.at[slot], wgu_sem.at[slot, 0]),
                pltpu.make_async_copy(wu_ref.at[:, cols], wubuf.at[slot], wgu_sem.at[slot, 1]))

    def wdn(j):
        n, slot = lax.rem(j, nn), lax.rem(j, 2)
        cols = pl.ds(pl.multiple_of(n * TN, TN), TN)
        return pltpu.make_async_copy(wd_ref.at[:, cols], wdbuf.at[slot], wd_sem.at[slot])

    def y_out(n):
        cols = pl.ds(pl.multiple_of(n * TN, TN), TN)
        return pltpu.make_async_copy(sbuf.at[0, n], y_ref.at[:, cols], y_sem.at[n])

    for d in (0, 1):
        ag(0, d, first=True).start()
    for copy in wgu(0):
        copy.start()
    wdn(0).start()

    def step(s, carry):
        @pl.when(s < RING)
        def _():
            for d in (0, 1):
                ag(s - 1, d, first=True).wait_recv()

                @pl.when(s < RING - 1)
                def _():
                    ag(s, d).start()
            xd(s).start()
            pltpu.make_async_copy(xg_ref.at[s - 1, pl.ds(0, rows)], xbuf.at[pl.ds(0, rows)], x_sem.at[0]).start()

        @pl.when(s == RING)
        def _():
            xd(s, own=True).start()
            pltpu.make_async_copy(x_ref, xbuf.at[pl.ds(0, rows)], x_sem.at[0]).start()

        xd(s).wait_recv()
        theirs = pltpu.make_async_copy(
            xg_ref.at[s - 1, pl.ds(rows, rows)], xbuf.at[pl.ds(rows, rows)], x_sem.at[1])
        theirs.start()
        pltpu.make_async_copy(xg_ref.at[s - 1, pl.ds(0, rows)], xbuf.at[pl.ds(0, rows)], x_sem.at[0]).wait()
        theirs.wait()

        def gate_up(t, carry):
            i = (s - 1) * nf + t

            @pl.when(i + 1 < RING * nf)
            def _():
                for copy in wgu(i + 1):
                    copy.start()
            for copy in wgu(i):
                copy.wait()
            slot = lax.rem(i, 2)
            gate = jnp.dot(xbuf[...], wgbuf[slot], preferred_element_type=F32)
            up = jnp.dot(xbuf[...], wubuf[slot], preferred_element_type=F32)
            hid[t] = (jax.nn.silu(gate) * up).astype(BF16)
            return carry

        lax.fori_loop(0, nf, gate_up, 0)

        def combine(n):
            k = lax.rem(n, 2)

            @pl.when(s > 1)
            def _():
                for d in (0, 1):
                    rs_in(s, n, d).wait_recv()
                acc[k] = acc[k] + rs[lax.rem(s, 3), n].astype(F32)

            @pl.when((s > 2))
            def _():
                for d in (0, 1):
                    rsc(s - 2, n, d).wait_send()
            dd(n).wait_recv()
            sbuf[lax.rem(s, 2), n] = (acc[k] + d2d[n].astype(F32)).astype(BF16)

            @pl.when(s < RING)
            def _():
                for d in (0, 1):
                    rsc(s, n, d).start()

            @pl.when(s == RING)
            def _():
                y_out(n).start()

        def down(n, carry):
            j = (s - 1) * nn + n

            @pl.when(j + 1 < RING * nn)
            def _():
                wdn(j + 1).start()
            wdn(j).wait()
            slot = lax.rem(j, 2)
            term = jnp.dot(hid[0], wdbuf[slot, 0:TF], preferred_element_type=F32)
            for t in range(1, nf):
                term += jnp.dot(hid[t], wdbuf[slot, t * TF:(t + 1) * TF], preferred_element_type=F32)
            acc[lax.rem(n, 2)] = term[:rows]

            @pl.when(s > 1)
            def _():
                dd(n).wait_send()
            pbuf[n] = term[rows:].astype(BF16)
            dd(n).start()

            @pl.when(n > 0)
            def _():
                combine(n - 1)
            return carry

        lax.fori_loop(0, nn, down, 0)
        combine(nn - 1)
        return carry

    lax.fori_loop(1, RING + 1, step, 0)

    def drain(n, carry):
        y_out(n).wait()
        dd(n).wait_send()
        for d in (0, 1):
            rsc(RING - 1, n, d).wait_send()
        return carry

    lax.fori_loop(0, nn, drain, 0)
    for s in range(RING):
        xd(s + 1).wait_send()
        if s < RING - 1:
            for d in (0, 1):
                ag(s, d, first=s == 0).wait_send()


def solution(mesh):
    def step(x, w_gate, w_up, w_down):
        rows, dim = x.shape
        ff = w_gate.shape[1]
        nn = dim // TN
        hbm = pl.BlockSpec(memory_space=pl.ANY)
        dma = pltpu.SemaphoreType.DMA
        out, _ = pl.pallas_call(
            kernel,
            out_shape=(
                jax.ShapeDtypeStruct((rows, dim), BF16),
                jax.ShapeDtypeStruct((RING, 2 * rows, dim), BF16),
            ),
            in_specs=[hbm] * 4,
            out_specs=(hbm, hbm),
            scratch_shapes=[
                pltpu.VMEM((2 * rows, dim), BF16),
                pltpu.VMEM((2, dim, TF), BF16),
                pltpu.VMEM((2, dim, TF), BF16),
                pltpu.VMEM((2, ff, TN), BF16),
                pltpu.VMEM((ff // TF, 2 * rows, TF), BF16),
                pltpu.VMEM((2, rows, TN), F32),
                pltpu.VMEM((3, nn, rows, TN), BF16),
                pltpu.VMEM((nn, rows, TN), BF16),
                pltpu.VMEM((nn, rows, TN), BF16),
                pltpu.VMEM((2, nn, rows, TN), BF16),
                dma((RING, 2)), dma((RING, 2)),
                dma((RING,)), dma((RING,)),
                dma((2, nn, 2)), dma((3, nn, 2)),
                dma((nn,)), dma((nn,)),
                dma((2,)), dma((2, 2)), dma((2,)), dma((nn,)),
            ],
            compiler_params=pltpu.CompilerParams(
                collective_id=0, has_side_effects=True, vmem_limit_bytes=62 * 1024 * 1024),
        )(x, w_gate, w_up, w_down)
        return out

    return jax.shard_map(
        step,
        mesh=mesh,
        in_specs=(P(("dp", "tp"), None), P(None, "tp"), P(None, "tp"), P("tp", None)),
        out_specs=P(("dp", "tp"), None),
        check_vma=False,
    )
```

time: 727 us -> 372 us (0.51)
  waiting for transfers between devices: 542 us -> 0 us
  Pallas kernels: 0 us -> 368 us
  matrix products: 172 us -> 0 us
  between operations: 13.4 us -> 0.01 us
    pallas_call x0 -> x1, Pallas kernels: none -> 368 us  [step(): pl.pallas_call(kernel, out_shape=(jax.ShapeDtypeStruct((rows, dim), BF16)...]
    reduce_scatter x1 -> x0, waiting for transfers between devices: 354 us -> none  [step(): return lax.psum_scatter(term, 'tp', scatter_dimension=0, tiled=True)]
    all_gather x1 -> x0, waiting for transfers between devices: 187 us -> none  [step(): rows = lax.all_gather(x, 'tp', axis=0, tiled=True)]
    dot_general x3 -> x0, matrix products: 172 us -> none  [the longest x1 57.9 us: step(): gate = jnp.dot(rows, w_gate, preferred_element_type=jnp.float32)]
  transfers between devices with their start and end apart: 2 -> 0, of which waited for: 2 -> 0; matrix products, arithmetic and copies ran while one was open for 0% -> 0% of each run, Pallas kernels for 0% -> 0%
where the time goes in v1:
time: 372 us; the launch traced here: 371 us
  Pallas kernels  368 us (99%)
    pallas_call x1, Pallas kernels, step(): pl.pallas_call(kernel, out_shape=(jax.ShapeDtypeStruct((rows, dim), BF16)...  368 us

profile of v1, /device:TPU:0, one launch (start us, length us, event | category | flops | bytes accessed | tf_op | source)
XLA Modules:
  0.0 370.7 jit_solution(17310196418088094623)
XLA Ops:
  0.0 367.5 %shard_map.46 = (bf16[160,7168]{1,0:T(8,128)(2,1)}, bf16[8,320,7168]{2,1,0:T(8,128)(2,1)}) custom-call(bf16[160,7168]{1,0:T(8,128)(2,1)} %x_ref.1, bf16[7168,1280]{1,0:T(8,128)(2,1)} %wg_ref.1, bf16[7168,1280]{1,0:T(8,128)(2,1)} %wu_ref.1, bf16[1280,7168]{1,0:T(8,128)(2,1)} %wd_ref.1), custom_call_target="tpu_custom_call" | custom-call | tf_op jit(solution)/shard_map/pallas_call | solution.py:208
  367.5 3.2 copy.6

commit v2 on v1

v2 whole, which is shorter than its diff:
```python
import jax
import jax.numpy as jnp
from jax import lax
from jax.experimental import pallas as pl
from jax.experimental.pallas import tpu as pltpu
from jax.sharding import PartitionSpec as P

MESH = pl.DeviceIdType.MESH
F32 = jnp.float32
BF16 = jnp.bfloat16
RING = 8
TF = 256
TN = 1024
EARLY = 2
SLOTS = 4


def chip_at(place):
    y = lax.div(place, 4)
    along = lax.rem(place, 4)
    return 4 * y + along + y * (3 - 2 * along)


def kernel(x_ref, wg_ref, wu_ref, wd_ref, y_ref, xg_ref, xbuf, wgbuf, wubuf, wdbuf, hid, acc, own, rs, d2d, pbuf, sbuf,
           ag_send, ag_recv, xd_send, xd_recv, rs_send, rs_recv, dd_send, dd_recv, x_sem, wgu_sem, wd_sem, y_sem):
    rows = x_ref.shape[0]
    half = rows // 2
    nf = wg_ref.shape[1] // TF
    nn = wd_ref.shape[1] // TN
    me = lax.axis_index("tp")
    chip = lax.div(me, 2)
    core = lax.rem(me, 2)
    y, z = lax.div(chip, 4), lax.rem(chip, 4)
    place = z + y * (7 - 2 * z)
    nxt = chip_at(lax.rem(place + 1, RING)) * 2 + core
    prv = chip_at(lax.rem(place + RING - 1, RING)) * 2 + core
    partner = chip * 2 + 1 - core
    to = (nxt, prv)

    barrier = pltpu.get_barrier_semaphore()
    for other in (nxt, prv, partner):
        pl.semaphore_signal(barrier, inc=1, device_id={"tp": other}, device_id_type=MESH)
    pl.semaphore_wait(barrier, 3)

    def part(d):
        return pl.ds(d * half, half)

    def remote(src, dst, send, recv, dev):
        return pltpu.make_async_remote_copy(
            src_ref=src, dst_ref=dst, send_sem=send, recv_sem=recv, device_id={"tp": dev}, device_id_type=MESH)

    def ag(s, d, p, first=False):
        piece = pl.ds(d * half + p * (half // 2), half // 2)
        src = x_ref.at[piece] if first else xg_ref.at[s - 1, piece]
        k = d * 2 + p
        return remote(src, xg_ref.at[s, piece], ag_send.at[s, k], ag_recv.at[s, k], to[d])

    def xd(s, own=False):
        k = lax.rem(s + RING - 1, RING)
        src = x_ref if own else xg_ref.at[k, pl.ds(0, rows)]
        return remote(src, xg_ref.at[k, pl.ds(rows, rows)], xd_send.at[k], xd_recv.at[k], partner)

    def rsc(s, n, d):
        return remote(sbuf.at[lax.rem(s, 2), n, part(d)], rs.at[lax.rem(s + 1, SLOTS), n, part(d)],
                      rs_send.at[lax.rem(s, 2), n, d], rs_recv.at[lax.rem(s + 1, SLOTS), n, d], to[d])

    def rs_in(s, n, d):
        return remote(sbuf.at[0, n, part(d)], rs.at[lax.rem(s, SLOTS), n, part(d)],
                      rs_send.at[0, n, d], rs_recv.at[lax.rem(s, SLOTS), n, d], to[d])

    def dd(s, n):
        slot = lax.rem(s, 2)
        return remote(pbuf.at[n], d2d.at[slot, n], dd_send.at[n], dd_recv.at[slot, n], partner)

    def wgu(i):
        t, slot = lax.rem(i, nf), lax.rem(i, 2)
        cols = pl.ds(pl.multiple_of(t * TF, TF), TF)
        return (pltpu.make_async_copy(wg_ref.at[:, cols], wgbuf.at[slot], wgu_sem.at[slot, 0]),
                pltpu.make_async_copy(wu_ref.at[:, cols], wubuf.at[slot], wgu_sem.at[slot, 1]))

    def wdn(j):
        n, slot = lax.rem(j, nn), lax.rem(j, 2)
        cols = pl.ds(pl.multiple_of(n * TN, TN), TN)
        return pltpu.make_async_copy(wd_ref.at[:, cols], wdbuf.at[slot], wd_sem.at[slot])

    def y_out(n):
        cols = pl.ds(pl.multiple_of(n * TN, TN), TN)
        return pltpu.make_async_copy(sbuf.at[0, n], y_ref.at[:, cols], y_sem.at[n])

    for p in (0, 1):
        for d in (0, 1):
            ag(0, d, p, first=True).start()
    for copy in wgu(0):
        copy.start()
    wdn(0).start()

    def x_mine(s):
        return pltpu.make_async_copy(xg_ref.at[s - 1, pl.ds(0, rows)], xbuf.at[pl.ds(0, rows)], x_sem.at[0])

    def x_theirs(s):
        k = lax.rem(s + RING - 1, RING)
        return pltpu.make_async_copy(xg_ref.at[k, pl.ds(rows, rows)], xbuf.at[pl.ds(rows, rows)], x_sem.at[1])

    def onward(s, p):
        for d in (0, 1):
            ag(s - 1, d, p, first=True).wait_recv()

            @pl.when(s < RING - 1)
            def _():
                ag(s, d, p).start()

    def arrive(s):
        @pl.when(s > EARLY)
        def _():
            onward(s, 0)
        onward(s, 1)
        xd(s).start()
        x_mine(s).start()

    xd(0, own=True).start()
    pltpu.make_async_copy(x_ref, xbuf.at[pl.ds(0, rows)], x_sem.at[0]).start()
    xd(0, own=True).wait_recv()
    x_theirs(0).start()

    def step(s, carry):
        pltpu.make_async_copy(x_ref, xbuf.at[pl.ds(0, rows)], x_sem.at[0]).wait()
        x_theirs(s).wait()

        def gate_up(t, carry):
            i = s * nf + t

            @pl.when(i + 1 < RING * nf)
            def _():
                for copy in wgu(i + 1):
                    copy.start()
            for copy in wgu(i):
                copy.wait()
            slot = lax.rem(i, 2)

            @pl.when((s < EARLY) & (t == nf - 3))
            def _():
                onward(s + 1, 0)
            gate = jnp.dot(xbuf[...], wgbuf[slot], preferred_element_type=F32)
            up = jnp.dot(xbuf[...], wubuf[slot], preferred_element_type=F32)
            hid[t] = (jax.nn.silu(gate) * up).astype(BF16)
            return carry

        lax.fori_loop(0, nf, gate_up, 0)

        def combine(n):
            k = lax.rem(n, 2)
            dd(s, n).wait_recv()

            @pl.when(s == 0)
            def _():
                own[n] = acc[k] + d2d[lax.rem(s, 2), n].astype(F32)

            @pl.when(s > 1)
            def _():
                for d in (0, 1):
                    rs_in(s, n, d).wait_recv()
                acc[k] = acc[k] + rs[lax.rem(s, SLOTS), n].astype(F32)

            @pl.when(s > 2)
            def _():
                for d in (0, 1):
                    rsc(s - 2, n, d).wait_send()

            @pl.when(s > 0)
            def _():
                sbuf[lax.rem(s, 2), n] = (acc[k] + d2d[lax.rem(s, 2), n].astype(F32)).astype(BF16)
                for d in (0, 1):
                    rsc(s, n, d).start()

        def down(n, carry):
            j = s * nn + n

            @pl.when(j + 1 < RING * nn)
            def _():
                wdn(j + 1).start()
            wdn(j).wait()
            slot = lax.rem(j, 2)
            term = jnp.dot(hid[0], wdbuf[slot, 0:TF], preferred_element_type=F32)
            for t in range(1, nf):
                term += jnp.dot(hid[t], wdbuf[slot, t * TF:(t + 1) * TF], preferred_element_type=F32)
            acc[lax.rem(n, 2)] = term[:rows]

            @pl.when(s > 0)
            def _():
                dd(s, n).wait_send()
            pbuf[n] = term[rows:].astype(BF16)
            dd(s, n).start()

            @pl.when(n > 0)
            def _():
                combine(n - 1)

            @pl.when((s < RING - 1) & (n == nn - 3))
            def _():
                xd(s + 1).wait_recv()
                x_theirs(s + 1).start()
            return carry

        @pl.when(s < RING - 1)
        def _():
            arrive(s + 1)

        lax.fori_loop(0, nn, down, 0)
        combine(nn - 1)
        return carry

    lax.fori_loop(0, RING, step, 0)

    def finish(n, carry):
        for d in (0, 1):
            rsc(RING - 2, n, d).wait_send()
            rs_in(RING, n, d).wait_recv()
        sbuf[0, n] = (own[n] + rs[RING % SLOTS, n].astype(F32)).astype(BF16)
        y_out(n).start()
        return carry

    lax.fori_loop(0, nn, finish, 0)

    def drain(n, carry):
        y_out(n).wait()
        dd(0, n).wait_send()
        for d in (0, 1):
            rsc(RING - 1, n, d).wait_send()
        return carry

    lax.fori_loop(0, nn, drain, 0)
    for s in range(RING):
        xd(s).wait_send()
        if s < RING - 1:
            for d in (0, 1):
                for p in (0, 1):
                    ag(s, d, p, first=s == 0).wait_send()


def solution(mesh):
    def step(x, w_gate, w_up, w_down):
        rows, dim = x.shape
        ff = w_gate.shape[1]
        nn = dim // TN
        hbm = pl.BlockSpec(memory_space=pl.ANY)
        dma = pltpu.SemaphoreType.DMA
        out, _ = pl.pallas_call(
            kernel,
            out_shape=(
                jax.ShapeDtypeStruct((rows, dim), BF16),
                jax.ShapeDtypeStruct((RING, 2 * rows, dim), BF16),
            ),
            in_specs=[hbm] * 4,
            out_specs=(hbm, hbm),
            scratch_shapes=[
                pltpu.VMEM((2 * rows, dim), BF16),
                pltpu.VMEM((2, dim, TF), BF16),
                pltpu.VMEM((2, dim, TF), BF16),
                pltpu.VMEM((2, ff, TN), BF16),
                pltpu.VMEM((ff // TF, 2 * rows, TF), BF16),
                pltpu.VMEM((2, rows, TN), F32),
                pltpu.VMEM((nn, rows, TN), F32),
                pltpu.VMEM((SLOTS, nn, rows, TN), BF16),
                pltpu.VMEM((2, nn, rows, TN), BF16),
                pltpu.VMEM((nn, rows, TN), BF16),
                pltpu.VMEM((2, nn, rows, TN), BF16),
                dma((RING, 4)), dma((RING, 4)),
                dma((RING,)), dma((RING,)),
                dma((2, nn, 2)), dma((SLOTS, nn, 2)),
                dma((nn,)), dma((2, nn)),
                dma((2,)), dma((2, 2)), dma((2,)), dma((nn,)),
            ],
            compiler_params=pltpu.CompilerParams(
                collective_id=0, has_side_effects=True, vmem_limit_bytes=62 * 1024 * 1024),
        )(x, w_gate, w_up, w_down)
        return out

    return jax.shard_map(
        step,
        mesh=mesh,
        in_specs=(P(("dp", "tp"), None), P(None, "tp"), P(None, "tp"), P("tp", None)),
        out_specs=P(("dp", "tp"), None),
        check_vma=False,
    )
```

time: 372 us -> 356 us (0.957)
  Pallas kernels: 368 us -> 352 us
    pallas_call x1, Pallas kernels: 368 us -> 352 us  [step(): pl.pallas_call(kernel, out_shape=(jax.ShapeDtypeStruct((rows, dim), BF16)...]
where the time goes in v2:
time: 356 us; the launch traced here: 355 us
  Pallas kernels  352 us (99%)
    pallas_call x1, Pallas kernels, step(): pl.pallas_call(kernel, out_shape=(jax.ShapeDtypeStruct((rows, dim), BF16)...  352 us

profile of v2, /device:TPU:0, one launch (start us, length us, event | category | flops | bytes accessed | tf_op | source)
XLA Modules:
  0.0 355.0 jit_solution(5831547198524264350)
XLA Ops:
  0.0 351.8 %shard_map.46 = (bf16[160,7168]{1,0:T(8,128)(2,1)}, bf16[8,320,7168]{2,1,0:T(8,128)(2,1)}) custom-call(bf16[160,7168]{1,0:T(8,128)(2,1)} %x_ref.1, bf16[7168,1280]{1,0:T(8,128)(2,1)} %wg_ref.1, bf16[7168,1280]{1,0:T(8,128)(2,1)} %wu_ref.1, bf16[1280,7168]{1,0:T(8,128)(2,1)} %wd_ref.1), custom_call_target="tpu_custom_call" | custom-call | tf_op jit(solution)/shard_map/pallas_call | solution.py:247
  351.8 3.2 copy.6

commit v3 on v2

--- a/solution.py
+++ b/solution.py
@@ -12,6 +12,7 @@
 TF = 256
 TN = 1024
 EARLY = 2
+LATE = 2
 SLOTS = 4
 
 
@@ -21,8 +22,8 @@
     return 4 * y + along + y * (3 - 2 * along)
 
 
-def kernel(x_ref, wg_ref, wu_ref, wd_ref, y_ref, xg_ref, xbuf, wgbuf, wubuf, wdbuf, hid, acc, own, rs, d2d, pbuf, sbuf,
-           ag_send, ag_recv, xd_send, xd_recv, rs_send, rs_recv, dd_send, dd_recv, x_sem, wgu_sem, wd_sem, y_sem):
+def kernel(x_ref, wg_ref, wu_ref, wd_ref, y_ref, xg_ref, xbuf, wgbuf, wubuf, wdbuf, hid, acc, own, rs, qb, d2d, pbuf, sbuf,
+           ag_send, ag_recv, xd_send, xd_recv, rs_send, rs_recv, dd_send, dd_recv, x_sem, wgu_sem, wd_sem, y_sem, cs_send, bk_send, q_recv):
     rows = x_ref.shape[0]
     half = rows // 2
     nf = wg_ref.shape[1] // TF
@@ -36,11 +37,23 @@
     prv = chip_at(lax.rem(place + RING - 1, RING)) * 2 + core
     partner = chip * 2 + 1 - core
     to = (nxt, prv)
+    cross = chip_at(RING - 1 - place) * 2 + core
+    role = lax.rem(place, 4)
+    rho = (role, 3 - role)
+    mid = (role == 1) | (role == 2)
 
     barrier = pltpu.get_barrier_semaphore()
     for other in (nxt, prv, partner):
         pl.semaphore_signal(barrier, inc=1, device_id={"tp": other}, device_id_type=MESH)
-    pl.semaphore_wait(barrier, 3)
+
+    @pl.when(mid)
+    def _():
+        pl.semaphore_signal(barrier, inc=1, device_id={"tp": cross}, device_id_type=MESH)
+        pl.semaphore_wait(barrier, 4)
+
+    @pl.when(jnp.logical_not(mid))
+    def _():
+        pl.semaphore_wait(barrier, 3)
 
     def part(d):
         return pl.ds(d * half, half)
@@ -55,6 +68,29 @@
         k = d * 2 + p
         return remote(src, xg_ref.at[s, piece], ag_send.at[s, k], ag_recv.at[s, k], to[d])
 
+    def skips(s, d):
+        r = rho[d]
+        return (((r == 0) & (s >= 2) & (s <= 5)) | ((r == 1) & (s >= 4) & (s <= 6))
+                | ((r == 3) & (s >= 3) & (s <= 4)))
+
+    def crosses(s, d):
+        return mid & (s <= rho[d] + 1)
+
+    def ag_cross(s, d, p, first=False):
+        piece = pl.ds(d * half + p * (half // 2), half // 2)
+        src = x_ref.at[piece] if first else xg_ref.at[s - 1, piece]
+        k = d * 2 + p
+        slot = s + 6 - 2 * rho[d]
+        return remote(src, xg_ref.at[slot, piece], cs_send.at[s, k], ag_recv.at[slot, k], cross)
+
+    def ag_back(s, d, p):
+        piece = pl.ds(d * half + p * (half // 2), half // 2)
+        k = d * 2 + p
+        return remote(xg_ref.at[s + 1, piece], xg_ref.at[s, piece], bk_send.at[s - 3, k], ag_recv.at[s, k], to[1 - d])
+
+    def taken(s, d):
+        return (rho[d] == 1) & (s >= 5) & (s <= 6)
+
     def xd(s, own=False):
         k = lax.rem(s + RING - 1, RING)
         src = x_ref if own else xg_ref.at[k, pl.ds(0, rows)]
@@ -67,6 +103,13 @@
     def rs_in(s, n, d):
         return remote(sbuf.at[0, n, part(d)], rs.at[lax.rem(s, SLOTS), n, part(d)],
                       rs_send.at[0, n, d], rs_recv.at[lax.rem(s, SLOTS), n, d], to[d])
+
+    def rs_cross(s, n, d):
+        return remote(sbuf.at[lax.rem(s, 2), n, part(d)], qb.at[s - 1, n],
+                      rs_send.at[lax.rem(s, 2), n, d], q_recv.at[s - 1, n], cross)
+
+    def q_in(s, n):
+        return remote(sbuf.at[0, n, part(0)], qb.at[s - 4, n], rs_send.at[0, n, 0], q_recv.at[s - 4, n], cross)
 
     def dd(s, n):
         slot = lax.rem(s, 2)
@@ -90,6 +133,11 @@
     for p in (0, 1):
         for d in (0, 1):
             ag(0, d, p, first=True).start()
+    for d in (0, 1):
+        @pl.when(rho[d] == 2)
+        def _():
+            for p in (0, 1):
+                ag_cross(0, d, p, first=True).start()
     for copy in wgu(0):
         copy.start()
     wdn(0).start()
@@ -103,11 +151,17 @@
 
     def onward(s, p):
         for d in (0, 1):
-            ag(s - 1, d, p, first=True).wait_recv()
-
-            @pl.when(s < RING - 1)
+            @pl.when(jnp.logical_not(taken(s, d)))
+            def _():
+                ag(s - 1, d, p, first=True).wait_recv()
+
+            @pl.when((s < RING - 1) & jnp.logical_not(skips(s, d)))
             def _():
                 ag(s, d, p).start()
+
+            @pl.when(crosses(s, d) & (rho[d] == 2))
+            def _():
+                ag_cross(s, d, p).start()
 
     def arrive(s):
         @pl.when(s > EARLY)
@@ -116,6 +170,22 @@
         onward(s, 1)
         xd(s).start()
         x_mine(s).start()
+        for d in (0, 1):
+            @pl.when((rho[d] == 1) & (s >= 3) & (s <= 4))
+            def _():
+                for p in (0, 1):
+                    ag(s + 1, d, p, first=True).wait_recv()
+                    ag_back(s, d, p).start()
+
+            @pl.when((rho[d] == 1) & (s == LATE))
+            def _():
+                for p in (0, 1):
+                    ag_cross(0, d, p, first=True).start()
+
+            @pl.when((rho[d] == 1) & (s > LATE) & (s <= LATE + 2))
+            def _():
+                for p in (0, 1):
+                    ag_cross(s - LATE, d, p).start()
 
     xd(0, own=True).start()
     pltpu.make_async_copy(x_ref, xbuf.at[pl.ds(0, rows)], x_sem.at[0]).start()
@@ -155,11 +225,18 @@
             def _():
                 own[n] = acc[k] + d2d[lax.rem(s, 2), n].astype(F32)
 
-            @pl.when(s > 1)
-            def _():
-                for d in (0, 1):
+            for d in (0, 1):
+                lines = slice(d * half, (d + 1) * half)
+
+                @pl.when((s > 1) & jnp.logical_not((rho[d] == 3) & (s <= 6)))
+                def _():
                     rs_in(s, n, d).wait_recv()
-                acc[k] = acc[k] + rs[lax.rem(s, SLOTS), n].astype(F32)
+                    acc[k, lines] = acc[k, lines] + rs[lax.rem(s, SLOTS), n, lines].astype(F32)
+
+                @pl.when((rho[d] == 1) & (s >= 4))
+                def _():
+                    q_in(s, n).wait_recv()
+                    acc[k, lines] = acc[k, lines] + qb[s - 4, n].astype(F32)
 
             @pl.when(s > 2)
             def _():
@@ -170,7 +247,15 @@
             def _():
                 sbuf[lax.rem(s, 2), n] = (acc[k] + d2d[lax.rem(s, 2), n].astype(F32)).astype(BF16)
                 for d in (0, 1):
-                    rsc(s, n, d).start()
+                    over = (rho[d] == 2) & (s <= 5)
+
+                    @pl.when(over)
+                    def _():
+                        rs_cross(s, n, d).start()
+
+                    @pl.when(jnp.logical_not(over))
+                    def _():
+                        rsc(s, n, d).start()
 
         def down(n, carry):
             j = s * nn + n
@@ -215,6 +300,12 @@
         for d in (0, 1):
             rsc(RING - 2, n, d).wait_send()
             rs_in(RING, n, d).wait_recv()
+            lines = slice(d * half, (d + 1) * half)
+
+            @pl.when(rho[d] == 1)
+            def _():
+                q_in(RING, n).wait_recv()
+                own[n, lines] = own[n, lines] + qb[RING - 4, n].astype(F32)
         sbuf[0, n] = (own[n] + rs[RING % SLOTS, n].astype(F32)).astype(BF16)
         y_out(n).start()
         return carry
@@ -229,12 +320,24 @@
         return carry
 
     lax.fori_loop(0, nn, drain, 0)
-    for s in range(RING):
+    def sent(s, carry):
         xd(s).wait_send()
-        if s < RING - 1:
-            for d in (0, 1):
-                for p in (0, 1):
-                    ag(s, d, p, first=s == 0).wait_send()
+        for d in (0, 1):
+            for p in (0, 1):
+                @pl.when((s < RING - 1) & jnp.logical_not(skips(s, d)))
+                def _():
+                    ag(s, d, p, first=True).wait_send()
+
+                @pl.when(crosses(s, d))
+                def _():
+                    ag_cross(s, d, p, first=True).wait_send()
+
+                @pl.when((rho[d] == 1) & (s >= 3) & (s <= 4))
+                def _():
+                    ag_back(s, d, p).wait_send()
+        return carry
+
+    lax.fori_loop(0, RING, sent, 0)
 
 
 def solution(mesh):
@@ -261,6 +364,7 @@
                 pltpu.VMEM((2, rows, TN), F32),
                 pltpu.VMEM((nn, rows, TN), F32),
                 pltpu.VMEM((SLOTS, nn, rows, TN), BF16),
+                pltpu.VMEM((5, nn, rows // 2, TN), BF16),
                 pltpu.VMEM((2, nn, rows, TN), BF16),
                 pltpu.VMEM((nn, rows, TN), BF16),
                 pltpu.VMEM((2, nn, rows, TN), BF16),
@@ -269,6 +373,7 @@
                 dma((2, nn, 2)), dma((SLOTS, nn, 2)),
                 dma((nn,)), dma((2, nn)),
                 dma((2,)), dma((2, 2)), dma((2,)), dma((nn,)),
+                dma((4, 4)), dma((2, 4)), dma((5, nn)),
             ],
             compiler_params=pltpu.CompilerParams(
                 collective_id=0, has_side_effects=True, vmem_limit_bytes=62 * 1024 * 1024),

time: 356 us -> 331 us (0.930)
  Pallas kernels: 352 us -> 326 us
    pallas_call x1, Pallas kernels: 352 us -> 326 us  [step(): pl.pallas_call(kernel, out_shape=(jax.ShapeDtypeStruct((rows, dim), BF16)...]
where the time goes in v3:
time: 331 us; the launch traced here: 330 us
  Pallas kernels  326 us (98%)
    pallas_call x1, Pallas kernels, step(): pl.pallas_call(kernel, out_shape=(jax.ShapeDtypeStruct((rows, dim), BF16)...  326 us

profile of v3, /device:TPU:0, one launch (start us, length us, event | category | flops | bytes accessed | tf_op | source)
XLA Modules:
  0.0 329.6 jit_solution(18412890026671477314)
XLA Ops:
  0.0 326.4 %shard_map.46 = (bf16[160,7168]{1,0:T(8,128)(2,1)}, bf16[8,320,7168]{2,1,0:T(8,128)(2,1)}) custom-call(bf16[160,7168]{1,0:T(8,128)(2,1)} %x_ref.1, bf16[7168,1280]{1,0:T(8,128)(2,1)} %wg_ref.1, bf16[7168,1280]{1,0:T(8,128)(2,1)} %wu_ref.1, bf16[1280,7168]{1,0:T(8,128)(2,1)} %wd_ref.1), custom_call_target="tpu_custom_call" | custom-call | tf_op jit(solution)/shard_map/pallas_call | solution.py:350
  326.4 3.2 copy.6
